TPU v7x, 32 devices: a whole 2x2x4 slice. The times are simulated.
32 devices in a mesh: vpair: 4 (over y, x), rank: 8 (over z, core).
Axes of the slice: x: 2, y: 2, z: 4, core: 2. Of those that a mesh axis runs over, the one named last changes fastest.
Arguments:
- amplitudes: bfloat16 [8, 1200, 1200], P(None, 'vpair', 'rank'), may hold values from -6 to 6
- factors: bfloat16 [1200, 8192], P('vpair', 'rank'), may hold values from -0.1875 to 0.1875
- kernel: bfloat16 [8192, 8192], P('vpair', 'rank'), may hold values from -0.875 to 0.875
- other_terms: float32 [8, 1200, 1200], P(None, 'vpair'), may hold values from -6 to 6
- virt_energy: float32 [1200], replicated, may hold values from 0.2 to 4
- pair_energy: float32 [8], replicated, may hold values from -3 to -0.5
Outputs:
- residual: float32 [8, 1200, 1200], P(None, 'vpair')
- update_rms: float32 [], replicated
All inputs are finite; a program needn't handle non-finite values.
Results may differ from a plain program's by a relative error of at most 0.0035.
Values may be sent and summed in bfloat16 or wider, within the bound.
A program may use at most 192 MiB of HBM per device.

v0:
```python
import jax
import jax.numpy as jnp
from jax import lax
from jax.sharding import PartitionSpec as P

epsilon = 1e-06


def shards(amplitudes, factors, kernel, other_terms, virt_energy, pair_energy):
    vpair_count = lax.axis_size("vpair")
    pair_count = amplitudes.shape[0]
    row_block = amplitudes.shape[1]
    col_block = amplitudes.shape[2]
    virt_count = row_block * vpair_count
    right_block = kernel.shape[1]
    factor_rows = lax.all_gather(factors, "rank", axis=1, tiled=True)
    factor_full = lax.all_gather(factor_rows, "vpair", axis=0, tiled=True)
    factor_cols = lax.dynamic_slice_in_dim(
        factor_full, lax.axis_index("rank") * right_block, right_block, 1
    )
    half_done = jnp.einsum(
        "ons,sh->onh",
        lax.all_gather(amplitudes, "rank", axis=2, tiled=True),
        factor_cols,
        preferred_element_type=jnp.float32,
    ).astype(jnp.bfloat16)
    kernel_sub = lax.all_to_all(kernel, "vpair", split_axis=1, concat_axis=0, tiled=True).astype(
        jnp.float32
    )
    coupled = jnp.einsum(
        "cp,icq->ipq",
        factor_full,
        lax.all_to_all(half_done, "vpair", split_axis=2, concat_axis=1, tiled=True),
        preferred_element_type=jnp.float32,
    )
    weighted = (kernel_sub[None] * coupled).astype(jnp.bfloat16)
    ladder_half = jnp.einsum(
        "ap,ipq->iaq", factor_full, weighted, preferred_element_type=jnp.float32
    ).astype(jnp.bfloat16)
    back_half = lax.all_to_all(ladder_half, "vpair", split_axis=1, concat_axis=2, tiled=True)
    partial_value = jnp.einsum(
        "iaq,bq->iab", back_half, factor_cols, preferred_element_type=jnp.float32
    )
    row_energy = lax.dynamic_slice_in_dim(
        virt_energy, lax.axis_index("vpair") * row_block, row_block, 0
    )
    ladder_share = lax.psum_scatter(partial_value, "rank", scatter_dimension=2, tiled=True)
    col_start = lax.axis_index("rank") * col_block
    own_terms = lax.dynamic_slice_in_dim(other_terms, col_start, col_block, 2)
    part_residual = own_terms + ladder_share
    col_energy = lax.dynamic_slice_in_dim(virt_energy, col_start, col_block, 0)
    denominator = row_energy[None, :, None] + col_energy[None, None, :] - pair_energy[:, None, None]
    update = part_residual / denominator
    squares = lax.psum(jnp.sum(update * update), ("vpair", "rank"))
    residual = lax.all_gather(part_residual, "rank", axis=2, tiled=True)
    update_rms = jnp.sqrt(squares / (pair_count * virt_count * virt_count) + epsilon)
    return (residual, update_rms)


def solution(mesh):
    placed = (
        P(None, "vpair", "rank"),
        P("vpair", "rank"),
        P("vpair", "rank"),
        P(None, "vpair", None),
        P(),
        P(),
    )
    return jax.shard_map(
        shards, mesh=mesh, in_specs=placed, out_specs=(P(None, "vpair", None), P()), check_vma=False
    )
```

profile of v0, /device:TPU:0, one launch (start us, length us, event | category | flops | bytes accessed | tf_op | source)
XLA Modules:
  0.0 988.1 jit_solution(17243260461475593939)
XLA Ops:
  7.2 0.0 all-gather.6.cloned.1.call-start
  7.2 0.7 all-gather.6.cloned.1.call-update
  7.9 0.0 all-gather.12.cloned.1.call-start
  7.9 58.1 %all-gather.6.cloned.1.call-done = bf16[300,8192]{1,0:T(8,128)(2,1)} async-done(((bf16[300,1024]{1,0:T(8,128)(2,1)}), bf16[300,8192]{1,0:T(8,128)(2,1)}) %all-gather.6.cloned.1.call-update) | async-done | bytes 4915216 | tf_op jit(solution)/shard_map/all_gather | solution.py:16
  66.1 0.0 all-gather.12.cloned.1.call-update
  66.1 0.0 all-gather.8.cloned.1.call-start
  66.2 0.7 all-gather.8.cloned.1.call-update
  66.8 6.6 copy.34
  73.4 5.2 all-to-all-start
  78.6 213.5 %all-gather.12.cloned.1.call-done = bf16[4,300,8192]{2,1,0:T(8,128)(2,1)} async-done(((bf16[1,300,8192]{2,1,0:T(8,128)(2,1)}), bf16[4,300,8192]{2,1,0:T(8,128)(2,1)}) %all-gather.12.cloned.1.call-update) | async-done | bytes 19660816 | tf_op jit(solution)/shard_map/all_gather | solution.py:17
  292.1 20.4 %reshape.49 = bf16[1200,8192]{1,0:T(8,128)(2,1)} reshape(bf16[4,300,8192]{2,1,0:T(8,128)(2,1)} %all-gather.12.cloned.1.call-done) | data formatting | bytes 39321600
  312.5 54.9 %all-gather.8.cloned.1.call-done = bf16[8,300,1200]{1,0,2:T(8,128)(2,1)} async-done(((bf16[8,300,150]{1,0,2:T(8,128)(2,1)}), bf16[8,300,1200]{1,0,2:T(8,128)(2,1)}) %all-gather.8.cloned.1.call-update) | async-done | bytes 5760016 | tf_op jit(solution)/shard_map/all_gather | solution.py:23
  367.5 12.2 %convert_bitcast_fusion.1 = bf16[8,300,1024]{2,1,0:T(8,128)(2,1)} fusion(bf16[8,300,1200]{1,0,2:T(8,128)(2,1)} %all-gather.8.cloned.1.call-done, bf16[1200,8192]{1,0:T(8,128)(2,1)} %reshape.49, s32[]{:T(128)S(6)} %select_n.11), kind=kOutput, calls=%fused_computation.9 | convolution fusion | flops 5900697600 | bytes 14745604 | tf_op jit(solution)/shard_map/ons,sh->onh/dot_general | solution.py:21
  379.7 8.6 copy.38
  388.3 0.0 all-to-all-done
  388.3 5.2 all-to-all-start.1
  393.6 0.6 reduce-scatter.2.cloned.1.call-start
  394.1 6.7 convert_bitcast_fusion
  400.8 8.7 copy.35
  409.5 8.9 copy.36
  418.4 19.5 %reshape.51 = bf16[1200,8192,1]{1,0,2:T(8,128)(2,1)} reshape(bf16[4,300,8192]{2,1,0:T(8,128)(2,1)} %all-gather.12.cloned.1.call-done) | data formatting | bytes 39321600
  437.9 26.2 %all-to-all-done.1 = bf16[8,300,1024]{1,0,2:T(8,128)(2,1)} async-done(((bf16[8,300,1024]{1,0,2:T(8,128)(2,1)}), bf16[8,300,1024]{1,0,2:T(8,128)(2,1)}, u32[]{:S(2)}, u32[]{:S(2)}) %all-to-all-start.1) | async-done | bytes 4915232 | tf_op jit(solution)/shard_map/all_to_all | solution.py:33
  464.1 12.8 %copy.51 = bf16[8,300,4,256]{3,2,0,1:T(4,128)(2,1)} copy(bf16[8,300,4,256]{1,0,3,2:T(8,128)(2,1)} %bitcast.6) | data formatting | bytes 9830400 | tf_op jit(solution)/shard_map/all_to_all | solution.py:33
  476.9 5.2 copy.40
  482.2 53.7 %fusion.39 = bf16[8,8192,256]{1,2,0:T(8,128)(2,1)} fusion(f32[8192,256]{0,1:T(8,128)} %copy.36, bf16[1200,8192,1]{1,0,2:T(8,128)(2,1)} %reshape.51, bf16[8,1200,256]{2,0,1:T(8,128)(2,1)} %bitcast.49), kind=kOutput, calls=%fused_computation.1.clone.clone.clone.clone.clone.clone.1 | convolution fusion | flops 40298872832 | bytes 66519040 | tf_op jit(solution)/shard_map/cp,icq->ipq/dot_general | solution.py:30
  535.9 51.8 %fusion.13 = bf16[8,1200,256]{2,1,0:T(8,128)(2,1)} fusion(bf16[1200,8192,1]{1,0,2:T(8,128)(2,1)} %reshape.51, bf16[8,8192,256]{1,2,0:T(8,128)(2,1)} %fusion.39), kind=kOutput, calls=%fused_computation.11 | convolution fusion | flops 40267776000 | bytes 58130432 | tf_op jit(solution)/shard_map/ap,ipq->iaq/dot_general | solution.py:37
  587.7 8.8 copy.43
  596.5 58.1 %all_to_all.49 = bf16[8,1200,256]{2,0,1:T(8,128)(2,1)S(1)} all-to-all(bf16[8,1200,256]{2,0,1:T(8,128)(2,1)S(1)} %copy.43), channel_id=1, replica_groups=mesh['vpair'=4,'rank'=8] {'vpair'}, dimensions={1} | all-to-all | bytes 9830400 | tf_op jit(solution)/shard_map/all_to_all | solution.py:40
  654.7 0.7 copy.55
  655.4 10.7 %fusion.20 = f32[8,300,1200]{2,0,1:T(8,128)} fusion(bf16[8,300,1024]{2,0,1:T(8,128)(2,1)S(1)} %bitcast.48, bf16[1200,8192]{1,0:T(8,128)(2,1)} %reshape.49, s32[]{:T(128)S(6)} %select_n.11), kind=kOutput, calls=%fused_computation.12 | convolution fusion | flops 5898240000 | bytes 18892804 | tf_op jit(solution)/shard_map/iaq,bq->iab/dot_general | solution.py:41
  666.0 14.2 %copy.46 = f32[8,300,1200]{1,0,2:T(8,128)} copy(f32[8,300,1200]{2,0,1:T(8,128)} %fusion.20) | data formatting | bytes 23040000 | tf_op jit(solution)/shard_map/iaq,bq->iab/dot_general | solution.py:41
  680.2 0.0 reduce-scatter.2.cloned.1.call-update
  680.2 0.0 copy-start
  680.2 0.0 all-gather.10.cloned.1.call-start
  680.3 0.8 dynamic_slice.15
  681.1 0.8 dynamic_slice.14
  681.8 3.5 constant_dynamic-slice_fusion
  685.3 1.9 copy.54
  687.2 0.1 broadcast_add_fusion
  687.3 139.5 %reduce-scatter.2.cloned.1.call-done = f32[8,300,150]{1,0,2:T(8,128)} async-done(((f32[8,300,1200]{1,0,2:T(8,128)}), f32[8,300,150]{1,0,2:T(8,128)}) %reduce-scatter.2.cloned.1.call-update) | async-done | bytes 1440016 | tf_op jit(solution)/shard_map/reduce_scatter | solution.py:47
  826.9 0.0 copy-done
  826.9 4.3 multiply_reduce_fusion
  831.2 0.0 all-gather.10.cloned.1.call-update
  831.2 43.4 %psum.7 = f32[]{:T(128)} all-reduce(f32[]{:T(128)} %get-tuple-element.10), channel_id=1, replica_groups=mesh['vpair'=4,'rank'=8] {'vpair','rank'}, use_global_device_ids=true, to_apply=%region_2.0 | all-reduce | flops 1 | bytes 8 | tf_op jit(solution)/shard_map/psum | solution.py:54
  875.3 90.0 %all-gather.10.cloned.1.call-done = f32[8,300,1200]{1,0,2:T(8,128)} async-done(((f32[8,300,150]{1,0,2:T(8,128)}), f32[8,300,1200]{1,0,2:T(8,128)}) %all-gather.10.cloned.1.call-update) | async-done | bytes 11520016 | tf_op jit(solution)/shard_map/all_gather | solution.py:55
  965.3 14.7 %copy.47 = f32[8,300,1200]{2,0,1:T(8,128)} copy(f32[8,300,1200]{1,0,2:T(8,128)} %all-gather.10.cloned.1.call-done) | data formatting | bytes 23040000
Async XLA Ops:
  7.2 58.9 %all-gather.6.cloned.1.call-start = ((), (), s32[]{:S(2)}) async-start(), calls=%async_computation.4 | async-start | bytes 5603328 | tf_op jit(solution)/shard_map/all_gather | solution.py:16
  7.9 284.2 %all-gather.12.cloned.1.call-start = ((), (), s32[]{:S(2)}) async-start(), calls=%async_computation.8 | async-start | bytes 24903680 | tf_op jit(solution)/shard_map/all_gather | solution.py:17
  66.1 301.4 %all-gather.8.cloned.1.call-start = ((), (), s32[]{:S(2)}) async-start(), calls=%async_computation.5 | async-start | bytes 8294400 | tf_op jit(solution)/shard_map/all_gather | solution.py:23
  73.4 314.9 %all-to-all-start = ((bf16[2048,4,256]{0,2,1:T(8,128)(2,1)}), bf16[2048,4,256]{0,2,1:T(8,128)(2,1)}, u32[]{:S(2)}, u32[]{:S(2)}) async-start(bf16[2048,4,256]{0,2,1:T(8,128)(2,1)} %bitcast.46), calls=%async_computation | async-start | bytes 8388608 | tf_op jit(solution)/shard_map/all_to_all | solution.py:27
  388.3 75.8 %all-to-all-start.1 = ((bf16[8,300,1024]{1,0,2:T(8,128)(2,1)}), bf16[8,300,1024]{1,0,2:T(8,128)(2,1)}, u32[]{:S(2)}, u32[]{:S(2)}) async-start(bf16[8,300,1024]{1,0,2:T(8,128)(2,1)} %copy.38), calls=%async_computation.1 | async-start | bytes 12582912 | tf_op jit(solution)/shard_map/all_to_all | solution.py:33
  393.6 433.3 %reduce-scatter.2.cloned.1.call-start = ((), (), s32[]{:S(2)}) async-start(), calls=%async_computation.6 | async-start | bytes 16588800 | tf_op jit(solution)/shard_map/reduce_scatter | solution.py:47
  680.2 146.6 %copy-start = (f32[8]{0:T(128)S(1)}, f32[8]{0:T(128)}, u32[]{:S(2)}) copy-start(f32[8]{0:T(128)} %param.11) | copy-start | bytes 100
  680.2 285.0 %all-gather.10.cloned.1.call-start = ((), (), s32[]{:S(2)}) async-start(), calls=%async_computation.7 | async-start | bytes 16588800 | tf_op jit(solution)/shard_map/all_gather | solution.py:55
Sparse Core Ops, SparseCore 0:
  9.6 56.4 all-gather.5
  67.9 224.1 all-gather.11
  293.8 73.6 all-gather.7
  680.4 146.4 reduce-scatter.1
  831.3 133.8 all-gather.9
where the time goes:
time: 995 us; the launch traced here: 988 us
  waiting for transfers between devices  584 us (59%)
  local copies, waits for them, and re-layouts  136 us (14%)
  matrix products  128 us (13%)
  blocking collectives  102 us (10%)
  between operations  16.1 us (2%)
  starting transfers between devices  11.2 us (1%)
  other arithmetic  11 us (1%)
    all_gather x1, waiting for transfers between devices, shards(): factor_full = lax.all_gather(factor_rows, 'vpair', axis=0, tiled=True)  214 us
    reduce_scatter x1, waiting for transfers between devices, shards(): lax.psum_scatter(partial_value, 'rank', scatter_dimension=2, tiled=True)  140 us
    all_gather x1, waiting for transfers between devices, shards(): residual = lax.all_gather(part_residual, 'rank', axis=2, tiled=True)  90 us
    unnamed x7, local copies, waits for them, and re-layouts  63 us
    all_to_all x1, blocking collectives, shards(): lax.all_to_all(ladder_half, 'vpair', split_axis=1, concat_axis=2, tiled=T...  58.1 us
    all_gather x1, waiting for transfers between devices, shards(): factor_rows = lax.all_gather(factors, 'rank', axis=1, tiled=True)  58.1 us
    all_gather x1, waiting for transfers between devices, shards(): lax.all_gather(amplitudes, 'rank', axis=2, tiled=True)  54.9 us
    dot_general x1, matrix products, shards(): jnp.einsum('cp,icq->ipq', factor_full, lax.all_to_all(half_done, 'vpair',...  53.7 us
  transfers between devices with their start and end apart: 7, of which 6 were waited for; matrix products, arithmetic and copies ran while one was open for 10% of the time, Pallas kernels for 0%

commit v1 on v0

--- a/solution.py
+++ b/solution.py
@@ -1,6 +1,10 @@
+import functools
+
 import jax
 import jax.numpy as jnp
 from jax import lax
+from jax.experimental import pallas as pl
+from jax.experimental.pallas import tpu as pltpu
 from jax.sharding import PartitionSpec as P
 
 epsilon = 1e-06
@@ -57,6 +61,236 @@
     return (residual, update_rms)
 
 
+def middle_kernel(
+    zs, own_ref, half_ref, kern_ref, out_ref, gath_ref, fbuf, fturn, acc, mine_sem, load_sem, recv, s1, s2, s3
+):
+    v = lax.axis_index("vpair")
+    r = lax.axis_index("rank")
+    y, x = v // 2, v % 2
+    z, core = r // 2, r % 2
+    vx, vy, vd = y * 2 + 1 - x, (1 - y) * 2 + x, (1 - y) * 2 + 1 - x
+    mate = z * 2 + 1 - core
+    pairs, rows, cols = acc.shape
+    depth = own_ref.shape[1]
+
+    def rank_at(k):
+        return ((z + k) % zs) * 2 + core
+
+    barrier = pltpu.get_barrier_semaphore()
+    peers = [(v, rank_at(k)) for k in range(1, zs)] + [(vx, r), (vy, r), (v, mate)]
+    for peer in peers:
+        pl.semaphore_signal(barrier, inc=1, device_id=peer, device_id_type=pl.DeviceIdType.MESH)
+    pl.semaphore_wait(barrier, len(peers))
+
+    started = []
+
+    def send(src, rr, vv, sem, to):
+        copy = pltpu.make_async_remote_copy(
+            src_ref=src,
+            dst_ref=gath_ref.at[rr, vv],
+            send_sem=sem,
+            recv_sem=recv.at[rr, vv],
+            device_id=to,
+            device_id_type=pl.DeviceIdType.MESH,
+        )
+        copy.start()
+        started.append(copy)
+
+    def arrived(rr, vv):
+        pltpu.make_async_copy(gath_ref.at[rr, vv], gath_ref.at[rr, vv], recv.at[rr, vv]).wait()
+
+    send(own_ref, r, v, s2.at[0, 0], (vx, r))
+    send(own_ref, r, v, s2.at[0, 1], (vy, r))
+    for k in range(1, zs):
+        send(own_ref, r, v, s1.at[k], (v, rank_at(k)))
+    send(own_ref, r, v, s3.at[0, 0], (v, mate))
+
+    def spread(k):
+        rr = rank_at(k)
+        arrived(rr, v)
+        shard = gath_ref.at[rr, v]
+        send(shard, rr, v, s2.at[k, 0], (vx, r))
+        send(shard, rr, v, s2.at[k, 1], (vy, r))
+        send(shard, rr, v, s3.at[k, 0], (v, mate))
+
+    def relay(k):
+        rr = rank_at(k)
+        odd = (rr // 2) % 2
+        arrived(rr, vx)
+        arrived(rr, vy)
+        via = (y + odd * (1 - 2 * y)) * 2 + x + (1 - odd) * (1 - 2 * x)
+        to = (y + (1 - odd) * (1 - 2 * y)) * 2 + x + odd * (1 - 2 * x)
+        send(gath_ref.at[rr, via], rr, via, s2.at[k, 2], (to, r))
+        send(gath_ref.at[rr, vx], rr, vx, s3.at[k, 1], (v, mate))
+        send(gath_ref.at[rr, vy], rr, vy, s3.at[k, 2], (v, mate))
+
+    def finish(k):
+        rr = rank_at(k)
+        arrived(rr, vd)
+        send(gath_ref.at[rr, vd], rr, vd, s3.at[k, 3], (v, mate))
+
+    def compute(slot, rr, first):
+        start = pl.multiple_of(rr * depth, depth)
+
+        @pl.loop(0, depth // 128)
+        def _(c):
+            piece = fbuf[slot, :, :, pl.ds(pl.multiple_of(c * 128, 128), 128)].reshape(rows, 128)
+            fturn[pl.ds(pl.multiple_of(c * 128, 128), 128), :] = piece.T
+
+        @pl.loop(0, pairs)
+        def _(i):
+            half = half_ref[:, i].reshape(rows, cols)
+            coupled = jnp.dot(fturn[...], half, preferred_element_type=jnp.float32)
+            weight = kern_ref[pl.ds(start, depth), :].astype(jnp.float32)
+            weighted = (weight * coupled).astype(jnp.bfloat16)
+            term = jnp.dot(
+                fbuf[slot].reshape(rows, depth), weighted, preferred_element_type=jnp.float32
+            )
+            if first:
+                acc[i] = term
+            else:
+                acc[i] += term
+
+    def fetch(slot, rr):
+        for j in range(4):
+            pltpu.make_async_copy(gath_ref.at[rr, j], fbuf.at[slot, j], load_sem.at[slot, j]).start()
+
+    def fetched(slot, rr):
+        for j in range(4):
+            pltpu.make_async_copy(gath_ref.at[rr, j], fbuf.at[slot, j], load_sem.at[slot, j]).wait()
+
+    stage = fbuf.at[1, 0]
+    into = pltpu.make_async_copy(own_ref, stage, mine_sem.at[0])
+    into.start()
+    into.wait()
+    back = pltpu.make_async_copy(stage, gath_ref.at[r, v], mine_sem.at[1])
+    back.start()
+    back.wait()
+
+    relay(0)
+    spread(1)
+    finish(0)
+    fetch(0, r)
+    relay(1)
+    fetched(0, r)
+    compute(0, r, True)
+    for k in range(zs):
+        other = ((z + k) % zs) * 2 + 1 - core
+        if k + 2 < zs:
+            spread(k + 2)
+        for at in (v, vx, vy, vd):
+            arrived(other, at)
+        fetch(1, other)
+        if k + 1 < zs:
+            finish(k + 1)
+            fetch(0, rank_at(k + 1))
+        fetched(1, other)
+        compute(1, other, False)
+        if k + 1 < zs:
+            if k + 2 < zs:
+                relay(k + 2)
+            fetched(0, rank_at(k + 1))
+            compute(0, rank_at(k + 1), False)
+    for i in range(pairs):
+        out_ref[:, i] = acc[i].reshape(4, rows // 4, cols).astype(jnp.bfloat16)
+    for copy in started:
+        copy.wait_send()
+
+
+def ladder_middle(factors_pad, half_sub, kernel_sub, rank_count):
+    count, pairs, block, cols = half_sub.shape
+    depth = factors_pad.shape[1]
+    rows = count * block
+    points = kernel_sub.shape[0]
+    zs = rank_count // 2
+    hbm = pl.BlockSpec(memory_space=pl.ANY)
+    vmem = pl.BlockSpec(memory_space=pltpu.VMEM)
+    return pl.pallas_call(
+        functools.partial(middle_kernel, zs),
+        out_shape=(
+            jax.ShapeDtypeStruct((count, pairs, block, cols), jnp.bfloat16),
+            jax.ShapeDtypeStruct((rank_count, count, block, depth), jnp.bfloat16),
+        ),
+        in_specs=[hbm, vmem, vmem],
+        out_specs=(vmem, hbm),
+        scratch_shapes=[
+            pltpu.VMEM((2, count, block, depth), jnp.bfloat16),
+            pltpu.VMEM((depth, rows), jnp.bfloat16),
+            pltpu.VMEM((pairs, rows, cols), jnp.float32),
+            pltpu.SemaphoreType.DMA((2,)),
+            pltpu.SemaphoreType.DMA((2, count)),
+            pltpu.SemaphoreType.DMA((rank_count, count)),
+            pltpu.SemaphoreType.DMA((zs,)),
+            pltpu.SemaphoreType.DMA((zs, 3)),
+            pltpu.SemaphoreType.DMA((zs, 4)),
+        ],
+        compiler_params=pltpu.CompilerParams(
+            collective_id=0, has_side_effects=True, vmem_limit_bytes=60 * 1024 * 1024
+        ),
+        cost_estimate=pl.CostEstimate(
+            flops=4 * pairs * points * rows * cols, bytes_accessed=4 * points * rows, transcendentals=0
+        ),
+    )(factors_pad, half_sub, kernel_sub)
+
+
+def fast_shards(amplitudes, factors, kernel, other_terms, virt_energy, pair_energy):
+    vpair_count = lax.axis_size("vpair")
+    rank_count = lax.axis_size("rank")
+    pair_count, row_block, _ = amplitudes.shape
+    virt_count = row_block * vpair_count
+    right_block = kernel.shape[1]
+    cols = right_block // vpair_count
+    block = -(-row_block // 64) * 64
+    factor_cols = lax.all_gather(factors, "vpair", axis=0, tiled=False)
+    amps = lax.all_gather(amplitudes, "rank", axis=2, tiled=True)
+    kernel_sub = lax.all_to_all(kernel, "vpair", split_axis=1, concat_axis=0, tiled=True)
+    factor_cols = factor_cols.reshape(virt_count, right_block)
+    half_done = jnp.einsum(
+        "ons,sh->onh", amps, factor_cols, preferred_element_type=jnp.float32
+    ).astype(jnp.bfloat16)
+    half_done = jnp.pad(half_done, ((0, 0), (0, block - row_block), (0, 0)))
+    half_done = half_done.reshape(pair_count, block, vpair_count, cols).transpose(2, 0, 1, 3)
+    half_sub = lax.all_to_all(half_done, "vpair", split_axis=0, concat_axis=0, tiled=True)
+    factors_pad = jnp.pad(factors, ((0, block - row_block), (0, 0)))
+    back, _ = ladder_middle(factors_pad, half_sub, kernel_sub, rank_count)
+    back = lax.all_to_all(back, "vpair", split_axis=0, concat_axis=0, tiled=True)
+    back = back[:, :, :row_block]
+    partial_value = jnp.einsum(
+        "viaq,bvq->iab",
+        back,
+        factor_cols.reshape(virt_count, vpair_count, cols),
+        preferred_element_type=jnp.float32,
+    )
+    ladder_own = lax.psum_scatter(partial_value, "rank", scatter_dimension=0, tiled=True)
+    ladder = lax.all_gather(ladder_own.astype(jnp.bfloat16), "rank", axis=0, tiled=True)
+    own = ladder_own.shape[0]
+    start = lax.axis_index("rank") * own
+    row_energy = lax.dynamic_slice_in_dim(
+        virt_energy, lax.axis_index("vpair") * row_block, row_block, 0
+    )
+    own_terms = lax.dynamic_slice_in_dim(other_terms, start, own, 0)
+    own_pairs = lax.dynamic_slice_in_dim(pair_energy, start, own, 0)
+    denominator = row_energy[None, :, None] + virt_energy[None, None, :] - own_pairs[:, None, None]
+    update = (own_terms + ladder_own) / denominator
+    squares = lax.psum(jnp.sum(update * update), ("vpair", "rank"))
+    residual = other_terms + ladder.astype(jnp.float32)
+    update_rms = jnp.sqrt(squares / (pair_count * virt_count * virt_count) + epsilon)
+    return (residual, update_rms)
+
+
+def pick(amplitudes, factors, kernel, other_terms, virt_energy, pair_energy):
+    vpair_count = lax.axis_size("vpair")
+    rank_count = lax.axis_size("rank")
+    fits = (
+        vpair_count == 4
+        and rank_count % 2 == 0
+        and amplitudes.shape[0] % rank_count == 0
+        and kernel.shape[1] % (128 * vpair_count) == 0
+    )
+    body = fast_shards if fits else shards
+    return body(amplitudes, factors, kernel, other_terms, virt_energy, pair_energy)
+
+
 def solution(mesh):
     placed = (
         P(None, "vpair", "rank"),
@@ -67,5 +301,5 @@
         P(),
     )
     return jax.shard_map(
-        shards, mesh=mesh, in_specs=placed, out_specs=(P(None, "vpair", None), P()), check_vma=False
-    )
+        pick, mesh=mesh, in_specs=placed, out_specs=(P(None, "vpair", None), P()), check_vma=False
+    )

time: 995 us -> 865 us (0.87)
  Pallas kernels: 0 us -> 248 us
  waiting for transfers between devices: 584 us -> 473 us
  matrix products: 128 us -> 22 us
  local copies, waits for them, and re-layouts: 136 us -> 30.8 us
  blocking collectives: 102 us -> 39.3 us
    pallas_call x0 -> x1, Pallas kernels: none -> 248 us  [ladder_middle(): pl.pallas_call(functools.partial(middle_kernel, zs), out_shape=(jax.Shape...]
    all_gather x4 -> x3, waiting for transfers between devices: 417 us -> 205 us  [the longest x1 73.8 us: fast_shards(): amps = lax.all_gather(amplitudes, 'rank', axis=2, tiled=True)]
    dot_general x4 -> x2, matrix products: 128 us -> 22 us  [the longest x1 11.9 us: fast_shards(): jnp.einsum('viaq,bvq->iab', back, factor_cols.reshape(virt_count, vpair_c...]
    all_to_all x2 -> x3, waiting for transfers between devices: 26.2 us -> 113 us  [the longest x1 58.2 us: fast_shards(): lax.all_to_all(half_done, 'vpair', split_axis=0, concat_axis=0, tiled=True)]
    all_to_all x1 -> x0, blocking collectives: 58.1 us -> none  [shards(): lax.all_to_all(ladder_half, 'vpair', split_axis=1, concat_axis=2, tiled=T...]
    unnamed x7 -> x12, local copies, waits for them, and re-layouts: 63 us -> 18.3 us
    convert_element_type x4 -> x0, local copies, waits for them, and re-layouts: 35.1 us -> none  [the longest x2 17.6 us: shards(): lax.all_to_all(kernel, 'vpair', split_axis=1, concat_axis=0, tiled=True)]
    unnamed x0 -> x1, other arithmetic: none -> 15 us
  transfers between devices with their start and end apart: 7 -> 7, of which waited for: 6 -> 6; matrix products, arithmetic and copies ran while one was open for 10% -> 3% of each run, Pallas kernels for 0% -> 0%
where the time goes in v1:
time: 865 us; the launch traced here: 864 us
  waiting for transfers between devices  473 us (55%)
  Pallas kernels  248 us (29%)
  blocking collectives  39.3 us (5%)
  local copies, waits for them, and re-layouts  30.8 us (4%)
  matrix products  22 us (3%)
  other arithmetic  19.3 us (2%)
  starting transfers between devices  16 us (2%)
  between operations  15.7 us (2%)
    pallas_call x1, Pallas kernels, ladder_middle(): pl.pallas_call(functools.partial(middle_kernel, zs), out_shape=(jax.Shape...  248 us
    reduce_scatter x1, waiting for transfers between devices, fast_shards(): lax.psum_scatter(partial_value, 'rank', scatter_dimension=0, tiled=True)  154 us
    all_gather x1, waiting for transfers between devices, fast_shards(): amps = lax.all_gather(amplitudes, 'rank', axis=2, tiled=True)  73.8 us
    all_gather x1, waiting for transfers between devices, fast_shards(): factor_cols = lax.all_gather(factors, 'vpair', axis=0, tiled=False)  68.8 us
    all_gather x1, waiting for transfers between devices, fast_shards(): lax.all_gather(ladder_own.astype(jnp.bfloat16), 'rank', axis=0, tiled=True)  62.1 us
    all_to_all x1, waiting for transfers between devices, fast_shards(): lax.all_to_all(half_done, 'vpair', split_axis=0, concat_axis=0, tiled=True)  58.2 us
    all_to_all x1, waiting for transfers between devices, fast_shards(): lax.all_to_all(back, 'vpair', split_axis=0, concat_axis=0, tiled=True)  54.5 us
    psum x1, blocking collectives, fast_shards(): squares = lax.psum(jnp.sum(update * update), ('vpair', 'rank'))  39.3 us
  transfers between devices with their start and end apart: 7, of which 6 were waited for; matrix products, arithmetic and copies ran while one was open for 3% of the time, Pallas kernels for 0%

profile of v1, /device:TPU:0, one launch (start us, length us, event | category | flops | bytes accessed | tf_op | source)
XLA Modules:
  0.0 864.1 jit_solution(11852893201818783589)
XLA Ops:
  7.2 0.0 all-gather.10.cloned.1.call-start
  7.2 0.7 all-gather.10.cloned.1.call-update
  7.9 0.0 all-gather.6.cloned.1.call-start
  7.9 0.7 all-gather.6.cloned.1.call-update
  8.6 4.5 copy.45
  13.2 5.2 all-to-all-start.1
  18.4 68.8 %all-gather.10.cloned.1.call-done = bf16[4,300,1024]{2,1,0:T(8,128)(2,1)} async-done(((bf16[1,300,1024]{2,1,0:T(8,128)(2,1)}), bf16[4,300,1024]{2,1,0:T(8,128)(2,1)}) %all-gather.10.cloned.1.call-update) | async-done | bytes 2457616 | tf_op jit(solution)/shard_map/all_gather | solution.py:244
  87.2 1.9 reshape.76
  89.1 73.8 %all-gather.6.cloned.1.call-done = bf16[8,300,1200]{1,0,2:T(8,128)(2,1)} async-done(((bf16[8,300,150]{1,0,2:T(8,128)(2,1)}), bf16[8,300,1200]{1,0,2:T(8,128)(2,1)}) %all-gather.6.cloned.1.call-update) | async-done | bytes 5760016 | tf_op jit(solution)/shard_map/all_gather | solution.py:245
  162.9 10.1 %fusion.3 = bf16[8,300,1024]{2,1,0:T(8,128)(2,1)S(1)} fusion(bf16[1200,1024,1]{1,0,2:T(8,128)(2,1)S(1)} %reshape.76, bf16[8,300,1200]{1,0,2:T(8,128)(2,1)} %all-gather.6.cloned.1.call-done), kind=kOutput, calls=%fused_computation.7 | convolution fusion | flops 5900697600 | bytes 13132800 | tf_op jit(solution)/shard_map/ons,sh->onh/dot_general | solution.py:248
  173.0 0.8 pad.9
  173.8 3.0 copy.44
  176.8 0.0 all-to-all-done.1
  176.8 0.0 copy-start.2
  176.8 5.4 all-to-all-start
  182.2 0.0 copy-done.2
  182.3 0.9 pad.8.own_ref
  183.2 58.2 %all-to-all-done.half_ref = bf16[4,8,320,256]{3,2,1,0:T(8,128)(2,1)} async-done(((bf16[4,8,320,256]{3,2,1,0:T(8,128)(2,1)}), bf16[4,8,320,256]{3,2,1,0:T(8,128)(2,1)}, u32[]{:S(2)}, u32[]{:S(2)}) %all-to-all-start) | async-done | bytes 5242912 | tf_op jit(solution)/shard_map/all_to_all | solution.py:253
  241.4 248.4 %shard_map.77 = (bf16[4,8,320,256]{3,2,1,0:T(8,128)(2,1)}, bf16[8,4,320,1024]{3,2,1,0:T(8,128)(2,1)}) custom-call(bf16[320,1024]{1,0:T(8,128)(2,1)} %pad.8.own_ref, bf16[4,8,320,256]{3,2,1,0:T(8,128)(2,1)} %all-to-all-done.half_ref, bf16[8192,256]{1,0:T(8,128)(2,1)} %bitcast.3.kern_ref), custom_call_target="tpu_custom_call" | custom-call | flops 85899345920 | bytes 41943040 | tf_op jit(solution)/shard_map/pallas_call | solution.py:208
  489.8 0.0 copy-start
  489.8 5.3 all-to-all-start.2
  495.1 0.0 reduce-scatter.2.cloned.1.call-start
  495.1 0.0 copy-done
  495.1 2.6 reshape_reshape.3
  497.7 54.5 %all-to-all-done.2 = bf16[4,8,320,256]{3,2,1,0:T(8,128)(2,1)} async-done(((bf16[4,8,320,256]{3,2,1,0:T(8,128)(2,1)}), bf16[4,8,320,256]{3,2,1,0:T(8,128)(2,1)}, u32[]{:S(2)}, u32[]{:S(2)}) %all-to-all-start.2) | async-done | bytes 5242912 | tf_op jit(solution)/shard_map/all_to_all | solution.py:256
  552.2 11.9 %convolution_bitcast_fusion = f32[8,300,1200]{2,1,0:T(8,128)} fusion(bf16[4,8,320,256]{3,2,1,0:T(8,128)(2,1)} %all-to-all-done.2, bf16[1200,4,256,1]{2,1,0,3:T(4,128)(2,1)} %bitcast.25), kind=kOutput, calls=%fused_computation.3 | convolution fusion | flops 5898240000 | bytes 18958336 | tf_op jit(solution)/shard_map/viaq,bvq->iab/dot_general | solution.py:258
  564.1 0.0 copy-start.4
  564.1 0.0 copy-start.3
  564.1 0.0 reduce-scatter.2.cloned.1.call-update
  564.1 0.0 all-gather.8.cloned.1.call-start
  564.2 153.8 %reduce-scatter.2.cloned.1.call-done = f32[1,300,1200]{2,1,0:T(8,128)} async-done(((f32[8,300,1200]{2,1,0:T(8,128)}), f32[1,300,1200]{2,1,0:T(8,128)}) %reduce-scatter.2.cloned.1.call-update) | async-done | bytes 1440016 | tf_op jit(solution)/shard_map/reduce_scatter | solution.py:264
  718.0 2.4 convert_element_type.14
  720.3 0.0 all-gather.8.cloned.1.call-update
  720.4 0.0 copy-done.4
  720.4 0.6 dynamic_slice.11
  721.0 0.0 copy-done.3
  721.0 0.1 dynamic_slice.10
  721.0 0.0 copy-start.1
  721.0 62.1 %all-gather.8.cloned.1.call-done = bf16[8,300,1200]{2,1,0:T(8,128)(2,1)} async-done(((bf16[1,300,1200]{2,1,0:T(8,128)(2,1)}), bf16[8,300,1200]{2,1,0:T(8,128)(2,1)}) %all-gather.8.cloned.1.call-update) | async-done | bytes 5760016 | tf_op jit(solution)/shard_map/all_gather | solution.py:265
  783.1 15.0 %fusion.7 = (f32[8,300,1200]{2,1,0:T(8,128)S(1)}, f32[8,300,1200]{2,1,0:T(8,128)}) fusion(f32[8,300,1200]{2,0,1:T(8,128)} %param.9, bf16[8,300,1200]{2,1,0:T(8,128)(2,1)} %all-gather.8.cloned.1.call-done), kind=kLoop, calls=%fused_computation.10 | loop fusion | flops 5760000 | bytes 40320000 | tf_op args[3]
  798.1 0.0 copy-done.1
  798.1 2.0 multiply_reduce_fusion
  800.1 39.3 %psum.7 = f32[]{:T(128)} all-reduce(f32[]{:T(128)} %multiply_reduce_fusion), channel_id=1, replica_groups=mesh['vpair'=4,'rank'=8] {'vpair','rank'}, use_global_device_ids=true, to_apply=%region_2.3 | all-reduce | flops 1 | bytes 8 | tf_op jit(solution)/shard_map/psum | solution.py:275
  840.1 16.3 %copy.28 = f32[8,300,1200]{2,0,1:T(8,128)} copy(f32[8,300,1200]{2,1,0:T(8,128)} %get-tuple-element.11) | data formatting | bytes 23040000
Async XLA Ops:
  7.2 80.0 %all-gather.10.cloned.1.call-start = ((), (), s32[]{:S(2)}) async-start(), calls=%async_computation.7 | async-start | bytes 3112960 | tf_op jit(solution)/shard_map/all_gather | solution.py:244
  7.9 155.0 %all-gather.6.cloned.1.call-start = ((), (), s32[]{:S(2)}) async-start(), calls=%async_computation.4 | async-start | bytes 8294400 | tf_op jit(solution)/shard_map/all_gather | solution.py:245
  13.2 163.7 %all-to-all-start.1 = ((bf16[2048,4,256]{2,0,1:T(8,128)(2,1)}), bf16[2048,4,256]{2,0,1:T(8,128)(2,1)}, u32[]{:S(2)}, u32[]{:S(2)}) async-start(bf16[2048,4,256]{2,0,1:T(8,128)(2,1)} %bitcast.22), calls=%async_computation.1 | async-start | bytes 8388608 | tf_op jit(solution)/shard_map/all_to_all | solution.py:246
  176.8 5.4 copy-start.2
  176.8 64.5 %all-to-all-start = ((bf16[4,8,320,256]{3,2,1,0:T(8,128)(2,1)}), bf16[4,8,320,256]{3,2,1,0:T(8,128)(2,1)}, u32[]{:S(2)}, u32[]{:S(2)}) async-start(bf16[4,8,320,256]{3,2,1,0:T(8,128)(2,1)} %bitcast.20), calls=%async_computation | async-start | bytes 10485760 | tf_op jit(solution)/shard_map/all_to_all | solution.py:253
  489.8 5.3 copy-start
  489.8 62.4 %all-to-all-start.2 = ((bf16[4,8,320,256]{3,2,1,0:T(8,128)(2,1)}), bf16[4,8,320,256]{3,2,1,0:T(8,128)(2,1)}, u32[]{:S(2)}, u32[]{:S(2)}) async-start(bf16[4,8,320,256]{3,2,1,0:T(8,128)(2,1)} %get-tuple-element.3), calls=%async_computation.2 | async-start | bytes 10485760 | tf_op jit(solution)/shard_map/all_to_all | solution.py:256
  495.1 222.9 %reduce-scatter.2.cloned.1.call-start = ((), (), s32[]{:S(2)}) async-start(), calls=%async_computation.5 | async-start | bytes 14008320 | tf_op jit(solution)/shard_map/reduce_scatter | solution.py:264
  564.1 156.2 %copy-start.4 = (f32[8]{0:T(128)S(1)}, f32[8]{0:T(128)}, u32[]{:S(2)}) copy-start(f32[8]{0:T(128)} %param.11) | copy-start | bytes 100
  564.1 156.8 %copy-start.3 = (f32[1200]{0:T(1024)S(1)}, f32[1200]{0:T(1024)}, u32[]{:S(2)}) copy-start(f32[1200]{0:T(1024)} %param.10) | copy-start | bytes 14404
  564.1 219.0 %all-gather.8.cloned.1.call-start = ((), (), s32[]{:S(2)}) async-start(), calls=%async_computation.6 | async-start | bytes 7004160 | tf_op jit(solution)/shard_map/all_gather | solution.py:265
  721.0 77.1 %copy-start.1 = (f32[1,300,1200]{2,1,0:T(8,128)S(1)}, f32[1,300,1200]{2,1,0:T(8,128)}, u32[]{:S(2)}) copy-start(f32[1,300,1200]{2,1,0:T(8,128)} %reduce-scatter.2.cloned.1.call-done) | copy-start | bytes 4320004
Sparse Core Ops, SparseCore 0:
  9.8 77.3 all-gather.9
  88.8 74.0 all-gather.5
  564.3 153.6 reduce-scatter.1
  720.5 62.6 all-gather.7

commit v2 on v1

--- a/solution.py
+++ b/solution.py
@@ -129,7 +129,7 @@
         arrived(rr, vd)
         send(gath_ref.at[rr, vd], rr, vd, s3.at[k, 3], (v, mate))
 
-    def compute(slot, rr, first):
+    def compute(slot, rr, first, tasks=()):
         start = pl.multiple_of(rr * depth, depth)
 
         @pl.loop(0, depth // 128)
@@ -137,8 +137,7 @@
             piece = fbuf[slot, :, :, pl.ds(pl.multiple_of(c * 128, 128), 128)].reshape(rows, 128)
             fturn[pl.ds(pl.multiple_of(c * 128, 128), 128), :] = piece.T
 
-        @pl.loop(0, pairs)
-        def _(i):
+        def one(i):
             half = half_ref[:, i].reshape(rows, cols)
             coupled = jnp.dot(fturn[...], half, preferred_element_type=jnp.float32)
             weight = kern_ref[pl.ds(start, depth), :].astype(jnp.float32)
@@ -151,6 +150,13 @@
             else:
                 acc[i] += term
 
+        pieces = 4
+        each = pairs // pieces
+        for piece in range(pieces):
+            if piece < len(tasks):
+                tasks[piece]()
+            pl.loop(piece * each, (piece + 1) * each)(one)
+
     def fetch(slot, rr):
         for j in range(4):
             pltpu.make_async_copy(gath_ref.at[rr, j], fbuf.at[slot, j], load_sem.at[slot, j]).start()
@@ -171,30 +177,167 @@
     spread(1)
     finish(0)
     fetch(0, r)
-    relay(1)
+    queue = []
+    for k in range(1, zs):
+        if k + 1 < zs:
+            queue.append(functools.partial(spread, k + 1))
+        queue.append(functools.partial(relay, k))
+        queue.append(functools.partial(finish, k))
     fetched(0, r)
-    compute(0, r, True)
+    compute(0, r, True, queue[:4])
+    queue = queue[4:]
     for k in range(zs):
         other = ((z + k) % zs) * 2 + 1 - core
-        if k + 2 < zs:
-            spread(k + 2)
         for at in (v, vx, vy, vd):
             arrived(other, at)
         fetch(1, other)
         if k + 1 < zs:
-            finish(k + 1)
             fetch(0, rank_at(k + 1))
         fetched(1, other)
-        compute(1, other, False)
+        compute(1, other, False, queue[:4])
+        queue = queue[4:]
         if k + 1 < zs:
-            if k + 2 < zs:
-                relay(k + 2)
             fetched(0, rank_at(k + 1))
-            compute(0, rank_at(k + 1), False)
+            compute(0, rank_at(k + 1), False, queue[:4])
+            queue = queue[4:]
     for i in range(pairs):
         out_ref[:, i] = acc[i].reshape(4, rows // 4, cols).astype(jnp.bfloat16)
     for copy in started:
         copy.wait_send()
+
+
+def front_kernel(zs, own_ref, amp_ref, cols_ref, amps_ref, mine_sem, cols_recv, amps_recv, cs, us, ds, ms, stage, hold):
+    v = lax.axis_index("vpair")
+    r = lax.axis_index("rank")
+    y, x = v // 2, v % 2
+    z, core = r // 2, r % 2
+    near = (y * 2 + 1 - x, (1 - y) * 2 + x, (1 - y) * 2 + 1 - x)
+    mate = z * 2 + 1 - core
+    mesh_ids = pl.DeviceIdType.MESH
+    has_up, has_down = z + 1 < zs, z >= 1
+    up_to, down_to = ((z + 1) % zs) * 2 + core, ((z + zs - 1) % zs) * 2 + core
+
+    barrier = pltpu.get_barrier_semaphore()
+    peers = [(at, r) for at in near] + [(v, mate), (v, up_to), (v, down_to)]
+    for peer in peers:
+        pl.semaphore_signal(barrier, inc=1, device_id=peer, device_id_type=mesh_ids)
+    pl.semaphore_wait(barrier, len(peers))
+
+    def cols_copy(j, at, to):
+        return pltpu.make_async_remote_copy(
+            src_ref=own_ref, dst_ref=cols_ref.at[at], send_sem=cs.at[j], recv_sem=cols_recv.at[at],
+            device_id=(to, r), device_id_type=mesh_ids,
+        )
+
+    def amps_copy(src, at, sem, to):
+        return pltpu.make_async_remote_copy(
+            src_ref=src, dst_ref=amps_ref.at[at], send_sem=sem, recv_sem=amps_recv.at[at],
+            device_id=(v, to), device_id_type=mesh_ids,
+        )
+
+    def amps_wait(at):
+        pltpu.make_async_copy(amps_ref.at[at], amps_ref.at[at], amps_recv.at[at]).wait()
+
+    @pl.when(has_up)
+    def _():
+        amps_copy(amp_ref, r, us.at[0], up_to).start()
+
+    @pl.when(has_down)
+    def _():
+        amps_copy(amp_ref, r, ds.at[0], down_to).start()
+
+    for j in range(3):
+        cols_copy(j, v, near[j]).start()
+    amps_copy(amp_ref, r, ms.at[0, 0], mate).start()
+    a = pltpu.make_async_copy(own_ref, stage, mine_sem.at[0])
+    b = pltpu.make_async_copy(amp_ref, hold, mine_sem.at[1])
+    a.start()
+    b.start()
+    a.wait()
+    b.wait()
+    c = pltpu.make_async_copy(stage, cols_ref.at[v], mine_sem.at[2])
+    d = pltpu.make_async_copy(hold, amps_ref.at[r], mine_sem.at[3])
+    c.start()
+    d.start()
+    c.wait()
+    d.wait()
+
+    for s in range(1, zs):
+        low, high = ((z + zs - s) % zs) * 2 + core, ((z + s) % zs) * 2 + core
+
+        @pl.when(z >= s)
+        def _():
+            amps_wait(low)
+            amps_copy(amps_ref.at[low], low, ms.at[s, 0], mate).start()
+
+            @pl.when(has_up)
+            def _():
+                amps_copy(amps_ref.at[low], low, us.at[s], up_to).start()
+
+        @pl.when(z + s < zs)
+        def _():
+            amps_wait(high)
+            amps_copy(amps_ref.at[high], high, ms.at[s, 1], mate).start()
+
+            @pl.when(has_down)
+            def _():
+                amps_copy(amps_ref.at[high], high, ds.at[s], down_to).start()
+
+    for at in near:
+        pltpu.make_async_copy(cols_ref.at[at], cols_ref.at[at], cols_recv.at[at]).wait()
+    for k in range(zs):
+        amps_wait(k * 2 + 1 - core)
+    for j in range(3):
+        cols_copy(j, v, near[j]).wait_send()
+    amps_copy(amp_ref, r, ms.at[0, 0], mate).wait_send()
+    for s in range(zs):
+
+        @pl.when(jnp.logical_and(z >= s, has_up))
+        def _():
+            amps_copy(amp_ref, r, us.at[s], up_to).wait_send()
+
+        @pl.when(jnp.logical_and(z + s < zs, has_down))
+        def _():
+            amps_copy(amp_ref, r, ds.at[s], down_to).wait_send()
+
+        if s:
+
+            @pl.when(z >= s)
+            def _():
+                amps_copy(amp_ref, r, ms.at[s, 0], mate).wait_send()
+
+            @pl.when(z + s < zs)
+            def _():
+                amps_copy(amp_ref, r, ms.at[s, 1], mate).wait_send()
+
+
+def front_gather(factors_pad, amps_pad, vpair_count, rank_count):
+    zs = rank_count // 2
+    hbm = pl.BlockSpec(memory_space=pl.ANY)
+    return pl.pallas_call(
+        functools.partial(front_kernel, zs),
+        out_shape=(
+            jax.ShapeDtypeStruct((vpair_count, *factors_pad.shape), jnp.bfloat16),
+            jax.ShapeDtypeStruct((rank_count, *amps_pad.shape), jnp.bfloat16),
+        ),
+        in_specs=[hbm, hbm],
+        out_specs=(hbm, hbm),
+        scratch_shapes=[
+            pltpu.SemaphoreType.DMA((4,)),
+            pltpu.SemaphoreType.DMA((vpair_count,)),
+            pltpu.SemaphoreType.DMA((rank_count,)),
+            pltpu.SemaphoreType.DMA((3,)),
+            pltpu.SemaphoreType.DMA((zs,)),
+            pltpu.SemaphoreType.DMA((zs,)),
+            pltpu.SemaphoreType.DMA((zs, 2)),
+            pltpu.VMEM(factors_pad.shape, jnp.bfloat16),
+            pltpu.VMEM(amps_pad.shape, jnp.bfloat16),
+        ],
+        compiler_params=pltpu.CompilerParams(
+            collective_id=1, has_side_effects=True, vmem_limit_bytes=60 * 1024 * 1024
+        ),
+        cost_estimate=pl.CostEstimate(flops=10**10, bytes_accessed=10**7, transcendentals=0),
+    )(factors_pad, amps_pad)
 
 
 def ladder_middle(factors_pad, half_sub, kernel_sub, rank_count):
@@ -241,17 +384,26 @@
     right_block = kernel.shape[1]
     cols = right_block // vpair_count
     block = -(-row_block // 64) * 64
-    factor_cols = lax.all_gather(factors, "vpair", axis=0, tiled=False)
-    amps = lax.all_gather(amplitudes, "rank", axis=2, tiled=True)
+    col_block = amplitudes.shape[2]
+    deep = -(-col_block // 16) * 16
     kernel_sub = lax.all_to_all(kernel, "vpair", split_axis=1, concat_axis=0, tiled=True)
-    factor_cols = factor_cols.reshape(virt_count, right_block)
+    factors_pad = jnp.pad(factors, ((0, block - row_block), (0, 0)))
+    amps_pad = jnp.pad(
+        amplitudes.transpose(2, 0, 1), ((0, deep - col_block), (0, 0), (0, block - row_block))
+    ).reshape(deep, pair_count * block)
+    cols_pad, amps = front_gather(factors_pad, amps_pad, vpair_count, rank_count)
+    factor_cols = cols_pad[:, :row_block].reshape(virt_count, right_block)
+    cols_deep = jnp.pad(
+        factor_cols.reshape(rank_count, col_block, right_block), ((0, 0), (0, deep - col_block), (0, 0))
+    ).reshape(rank_count * deep, right_block)
     half_done = jnp.einsum(
-        "ons,sh->onh", amps, factor_cols, preferred_element_type=jnp.float32
+        "sm,sh->mh",
+        amps.reshape(rank_count * deep, pair_count * block),
+        cols_deep,
+        preferred_element_type=jnp.float32,
     ).astype(jnp.bfloat16)
-    half_done = jnp.pad(half_done, ((0, 0), (0, block - row_block), (0, 0)))
     half_done = half_done.reshape(pair_count, block, vpair_count, cols).transpose(2, 0, 1, 3)
     half_sub = lax.all_to_all(half_done, "vpair", split_axis=0, concat_axis=0, tiled=True)
-    factors_pad = jnp.pad(factors, ((0, block - row_block), (0, 0)))
     back, _ = ladder_middle(factors_pad, half_sub, kernel_sub, rank_count)
     back = lax.all_to_all(back, "vpair", split_axis=0, concat_axis=0, tiled=True)
     back = back[:, :, :row_block]
@@ -268,12 +420,14 @@
     row_energy = lax.dynamic_slice_in_dim(
         virt_energy, lax.axis_index("vpair") * row_block, row_block, 0
     )
-    own_terms = lax.dynamic_slice_in_dim(other_terms, start, own, 0)
+    own_terms = lax.optimization_barrier(lax.dynamic_slice_in_dim(other_terms, start, own, 0))
     own_pairs = lax.dynamic_slice_in_dim(pair_energy, start, own, 0)
     denominator = row_energy[None, :, None] + virt_energy[None, None, :] - own_pairs[:, None, None]
     update = (own_terms + ladder_own) / denominator
     squares = lax.psum(jnp.sum(update * update), ("vpair", "rank"))
-    residual = other_terms + ladder.astype(jnp.float32)
+    squares, ladder = lax.optimization_barrier((squares, ladder))
+    turned = lax.optimization_barrier(ladder.transpose(1, 0, 2))
+    residual = (other_terms.transpose(1, 0, 2) + turned.astype(jnp.float32)).transpose(1, 0, 2)
     update_rms = jnp.sqrt(squares / (pair_count * virt_count * virt_count) + epsilon)
     return (residual, update_rms)
 

time: 865 us -> 822 us (0.950)
  waiting for transfers between devices: 473 us -> 215 us
  Pallas kernels: 248 us -> 362 us
  blocking collectives: 39.3 us -> 108 us
  local copies, waits for them, and re-layouts: 30.8 us -> 60.5 us
    all_gather x2 -> x0, waiting for transfers between devices: 143 us -> none  [the longest x1 73.8 us: fast_shards(): amps = lax.all_gather(amplitudes, 'rank', axis=2, tiled=True)]
    pallas_call x0 -> x1, Pallas kernels: none -> 75.4 us  [front_gather(): pl.pallas_call(functools.partial(front_kernel, zs), out_shape=(jax.ShapeD...]
    all_to_all x0 -> x1, blocking collectives: none -> 65 us  [fast_shards(): lax.all_to_all(half_done, 'vpair', split_axis=0, concat_axis=0, tiled=True)]
    all_to_all x1 -> x0, waiting for transfers between devices: 58.2 us -> none  [fast_shards(): lax.all_to_all(half_done, 'vpair', split_axis=0, concat_axis=0, tiled=True)]
    all_gather x1, waiting for transfers between devices: 62.1 us -> 21.1 us  [fast_shards(): lax.all_gather(ladder_own.astype(jnp.bfloat16), 'rank', axis=0, tiled=True)]
    pallas_call x1, Pallas kernels: 248 us -> 287 us  [ladder_middle(): pl.pallas_call(functools.partial(middle_kernel, zs), out_shape=(jax.Shape...]
    unnamed x1 -> x0, other arithmetic: 15 us -> none
    transpose x0 -> x1, other arithmetic: none -> 14.8 us  [fast_shards(): (other_terms.transpose(1, 0, 2) + turned.astype(jnp.float32)).transpose(1...]
  transfers between devices with their start and end apart: 7 -> 4, of which waited for: 6 -> 3; matrix products, arithmetic and copies ran while one was open for 3% -> 6% of each run, Pallas kernels for 0% -> 9%
where the time goes in v2:
time: 822 us; the launch traced here: 816 us
  Pallas kernels  362 us (44%)
  waiting for transfers between devices  215 us (26%)
  blocking collectives  108 us (13%)
  local copies, waits for them, and re-layouts  60.5 us (7%)
  matrix products  24 us (3%)
  other arithmetic  19.5 us (2%)
  between operations  16.1 us (2%)
  starting transfers between devices  10.5 us (1%)
    pallas_call x1, Pallas kernels, ladder_middle(): pl.pallas_call(functools.partial(middle_kernel, zs), out_shape=(jax.Shape...  287 us
    reduce_scatter x1, waiting for transfers between devices, fast_shards(): lax.psum_scatter(partial_value, 'rank', scatter_dimension=0, tiled=True)  141 us
    pallas_call x1, Pallas kernels, front_gather(): pl.pallas_call(functools.partial(front_kernel, zs), out_shape=(jax.ShapeD...  75.4 us
    all_to_all x1, blocking collectives, fast_shards(): lax.all_to_all(half_done, 'vpair', split_axis=0, concat_axis=0, tiled=True)  65 us
    all_to_all x1, waiting for transfers between devices, fast_shards(): lax.all_to_all(back, 'vpair', split_axis=0, concat_axis=0, tiled=True)  52.7 us
    psum x1, blocking collectives, fast_shards(): squares = lax.psum(jnp.sum(update * update), ('vpair', 'rank'))  42.7 us
    unnamed x10, local copies, waits for them, and re-layouts  29.2 us
    all_gather x1, waiting for transfers between devices, fast_shards(): lax.all_gather(ladder_own.astype(jnp.bfloat16), 'rank', axis=0, tiled=True)  21.1 us
  transfers between devices with their start and end apart: 4, of which 3 were waited for; matrix products, arithmetic and copies ran while one was open for 6% of the time, Pallas kernels for 9%

profile of v2, /device:TPU:0, one launch (start us, length us, event | category | flops | bytes accessed | tf_op | source)
XLA Modules:
  0.0 815.8 jit_solution(7263429019054708823)
XLA Ops:
  7.2 4.5 copy.37
  11.7 0.0 copy-start.1
  11.7 0.0 copy-start
  11.7 5.3 all-to-all-start.1
  17.0 0.0 copy-done.1
  17.0 0.9 pad.12.own_ref
  17.9 0.0 copy-done
  17.9 0.1 pad.13
  18.0 1.5 reshape.70.amp_ref
  19.6 75.4 %shard_map.77 = (bf16[4,320,1024]{2,1,0:T(8,128)(2,1)}, bf16[8,160,2560]{2,1,0:T(8,128)(2,1)}) custom-call(bf16[320,1024]{1,0:T(8,128)(2,1)} %pad.12.own_ref, bf16[160,2560]{1,0:T(8,128)(2,1)} %reshape.70.amp_ref), custom_call_target="tpu_custom_call" | custom-call | flops 10000000000 | bytes 10000000 | tf_op jit(solution)/shard_map/pallas_call | solution.py:317
  95.0 1.9 slice.6
  97.0 2.2 reshape_reshape.6
  99.2 12.0 %bitcast_convert_fusion = bf16[2560,1024]{1,0:T(8,128)(2,1)} fusion(bf16[8,160,2560]{2,1,0:T(8,128)(2,1)} %get-tuple-element.7, bf16[8,150,1024]{2,1,0:T(8,128)(2,1)} %reshape_reshape.6), kind=kOutput, calls=%fused_computation.2 | convolution fusion | flops 6713507840 | bytes 14254080 | tf_op jit(solution)/shard_map/sm,sh->mh/dot_general | solution.py:399
  111.2 9.5 %reshape.71 = bf16[8,320,4,256]{3,2,1,0:T(4,128)(2,1)} reshape(bf16[2560,1024]{1,0:T(8,128)(2,1)} %bitcast_convert_fusion) | data formatting | bytes 10485760 | tf_op jit(solution)/shard_map/reshape | solution.py:405
  120.7 5.8 copy.36
  126.5 0.0 all-to-all-done.1
  126.5 65.0 %all_to_all.29.half_ref = bf16[4,8,320,256]{3,2,1,0:T(8,128)(2,1)} all-to-all(bf16[4,8,320,256]{3,2,1,0:T(8,128)(2,1)} %bitcast.25), channel_id=1, replica_groups=mesh['vpair'=4,'rank'=8] {'vpair'}, dimensions={0} | all-to-all | bytes 10485760 | tf_op jit(solution)/shard_map/all_to_all | solution.py:406
  191.5 286.8 %shard_map.78 = (bf16[4,8,320,256]{3,2,1,0:T(8,128)(2,1)}, bf16[8,4,320,1024]{3,2,1,0:T(8,128)(2,1)}) custom-call(bf16[320,1024]{1,0:T(8,128)(2,1)} %pad.12.own_ref, bf16[4,8,320,256]{3,2,1,0:T(8,128)(2,1)} %all_to_all.29.half_ref, bf16[8192,256]{1,0:T(8,128)(2,1)} %bitcast.5.kern_ref), custom_call_target="tpu_custom_call" | custom-call | flops 85899345920 | bytes 41943040 | tf_op jit(solution)/shard_map/pallas_call | solution.py:351
  478.3 5.1 all-to-all-start.2
  483.4 0.0 reduce-scatter.2.cloned.1.call-start
  483.4 2.6 reshape_reshape.7
  486.1 52.7 %all-to-all-done.2 = bf16[4,8,320,256]{3,2,1,0:T(8,128)(2,1)} async-done(((bf16[4,8,320,256]{3,2,1,0:T(8,128)(2,1)}), bf16[4,8,320,256]{3,2,1,0:T(8,128)(2,1)}, u32[]{:S(2)}, u32[]{:S(2)}) %all-to-all-start.2) | async-done | bytes 5242912 | tf_op jit(solution)/shard_map/all_to_all | solution.py:408
  538.8 12.0 %convolution_bitcast_fusion = f32[8,300,1200]{2,1,0:T(8,128)} fusion(bf16[4,8,320,256]{3,2,1,0:T(8,128)(2,1)} %all-to-all-done.2, bf16[1200,4,256,1]{2,1,0,3:T(4,128)(2,1)} %bitcast.29), kind=kOutput, calls=%fused_computation.3 | convolution fusion | flops 5898240000 | bytes 18958336 | tf_op jit(solution)/shard_map/viaq,bvq->iab/dot_general | solution.py:410
  550.7 0.0 reduce-scatter.2.cloned.1.call-update
  550.8 0.0 all-gather.2.cloned.1.call-start
  550.8 0.0 copy-start.3
  550.8 0.0 copy-start.2
  550.8 12.9 %copy.21 = f32[8,300,1200]{2,1,0:T(8,128)} copy(f32[8,300,1200]{2,0,1:T(8,128)} %param.9) | data formatting | bytes 23040000 | tf_op args[3]
  563.7 0.0 copy-done.3
  563.7 0.6 dynamic_slice.11
  564.3 1.5 constant_dynamic-slice_fusion
  565.8 0.0 copy-done.2
  565.8 0.1 dynamic_slice.10
  565.9 141.4 %reduce-scatter.2.cloned.1.call-done = f32[1,300,1200]{2,1,0:T(8,128)} async-done(((f32[8,300,1200]{2,1,0:T(8,128)}), f32[1,300,1200]{2,1,0:T(8,128)}) %reduce-scatter.2.cloned.1.call-update) | async-done | bytes 1440016 | tf_op jit(solution)/shard_map/reduce_scatter | solution.py:416
  707.2 4.8 fusion.5
  712.0 0.0 all-gather.2.cloned.1.call-update
  712.0 42.7 %psum.7 = f32[]{:T(128)} all-reduce(f32[]{:T(128)} %get-tuple-element.19), channel_id=1, replica_groups=mesh['vpair'=4,'rank'=8] {'vpair','rank'}, use_global_device_ids=true, to_apply=%region_2.3 | all-reduce | flops 1 | bytes 8 | tf_op jit(solution)/shard_map/psum | solution.py:427
  754.7 21.1 %all-gather.2.cloned.1.call-done = bf16[8,300,1200]{2,1,0:T(8,128)(2,1)} async-done(((bf16[1,300,1200]{2,1,0:T(8,128)(2,1)}), bf16[8,300,1200]{2,1,0:T(8,128)(2,1)}) %all-gather.2.cloned.1.call-update) | async-done | bytes 5760016 | tf_op jit(solution)/shard_map/all_gather | solution.py:417
  775.8 14.8 %fusion = f32[8,300,1200]{2,1,0:T(8,128)} fusion(bf16[300,8,1200]{2,0,1:T(8,128)(2,1)} %bitcast.27, f32[8,300,1200]{2,0,1:T(8,128)} %param.9), kind=kLoop, calls=%fused_computation.1 | loop fusion | flops 5760000 | bytes 28800000 | tf_op jit(solution)/shard_map/transpose | solution.py:430
  790.6 16.3 %copy.26 = f32[8,300,1200]{2,0,1:T(8,128)} copy(f32[8,300,1200]{2,1,0:T(8,128)} %fusion) | data formatting | bytes 23040000
Async XLA Ops:
  11.7 5.3 copy-start.1
  11.7 6.2 copy-start
  11.7 114.8 %all-to-all-start.1 = ((bf16[2048,4,256]{2,0,1:T(8,128)(2,1)}), bf16[2048,4,256]{2,0,1:T(8,128)(2,1)}, u32[]{:S(2)}, u32[]{:S(2)}) async-start(bf16[2048,4,256]{2,0,1:T(8,128)(2,1)} %bitcast.26), calls=%async_computation.1 | async-start | bytes 8388608 | tf_op jit(solution)/shard_map/all_to_all | solution.py:389
  478.3 60.5 %all-to-all-start.2 = ((bf16[4,8,320,256]{3,2,1,0:T(8,128)(2,1)}), bf16[4,8,320,256]{3,2,1,0:T(8,128)(2,1)}, u32[]{:S(2)}, u32[]{:S(2)}) async-start(bf16[4,8,320,256]{3,2,1,0:T(8,128)(2,1)} %get-tuple-element.9), calls=%async_computation.2 | async-start | bytes 10485760 | tf_op jit(solution)/shard_map/all_to_all | solution.py:408
  483.4 223.8 %reduce-scatter.2.cloned.1.call-start = ((), (), s32[]{:S(2)}) async-start(), calls=%async_computation.4 | async-start | bytes 14008320 | tf_op jit(solution)/shard_map/reduce_scatter | solution.py:416
  550.8 225.0 %all-gather.2.cloned.1.call-start = ((), (), s32[]{:S(2)}) async-start(), calls=%async_computation.5 | async-start | bytes 7004160 | tf_op jit(solution)/shard_map/all_gather | solution.py:417
  550.8 12.9 %copy-start.3 = (f32[8]{0:T(128)S(1)}, f32[8]{0:T(128)}, u32[]{:S(2)}) copy-start(f32[8]{0:T(128)} %param.11) | copy-start | bytes 100
  550.8 15.0 %copy-start.2 = (f32[1200]{0:T(1024)S(1)}, f32[1200]{0:T(1024)}, u32[]{:S(2)}) copy-start(f32[1200]{0:T(1024)} %param.10) | copy-start | bytes 14404
Sparse Core Ops, SparseCore 0:
  550.9 156.3 reduce-scatter.1
  712.2 63.6 all-gather.1
